TPU v7x, 32 devices: a whole 2x2x4 slice. The times are simulated.
32 devices in a mesh: ka: 4 (over z), row: 8 (over y, x, core).
Axes of the slice: x: 2, y: 2, z: 4, core: 2. Of those that a mesh axis runs over, the one named last changes fastest.
Arguments:
- hamiltonian: float32 [16384, 4096], P(('ka', 'row')), parts along dimension 0, as said below
Outputs:
- sign_next: float32 [16384, 4096], P(('ka', 'row')), parts along dimension 0
- occupation: float32 [4], P('ka'), parts along dimension 0
There are 4 independent parts, one for each index of `ka`. A program takes and returns all parts, laid end to end along the dimension named above; each array names one. Nothing has to cross between parts.
Inputs may be any that keep to these rules, and one draw needn't show every extreme that they name: hamiltonian is symmetric up to float32 rounding.
All inputs are finite; a program needn't handle non-finite values.
Results may differ from a plain program's by a relative error of at most 0.0038.
Values may be sent and summed in bfloat16 or wider, within the bound.
A program may use at most 128 MiB of HBM per device.

v0:
```python
from functools import partial
import jax
import jax.numpy as jnp
from jax import lax
from jax.sharding import PartitionSpec as P


def multiply_rows(left, gathered):
    return jnp.dot(left, gathered, preferred_element_type=jnp.float32)


def own_diagonal(matrix, position, block_rows, cycle_size):
    shaped = matrix.reshape(block_rows, cycle_size, block_rows)
    square_block = lax.dynamic_slice_in_dim(shaped, position, 1, 1)[:, 0, :]
    return jnp.sum(jnp.diagonal(square_block))


def shards(hamiltonian):
    cycle_size = lax.axis_size("row")
    position = lax.axis_index("row")
    block_rows, order = hamiltonian.shape
    rounded = hamiltonian.astype(jnp.bfloat16)
    gathered = lax.all_gather(rounded, "row", axis=0, tiled=True)
    multiply = partial(multiply_rows, gathered=gathered)
    square_low = multiply(rounded).astype(jnp.bfloat16)
    cube = multiply(square_low)
    sign_next = 1.5 * hamiltonian - 0.5 * cube
    total = lax.psum(own_diagonal(sign_next, position, block_rows, cycle_size), "row")
    occupation = jnp.reshape(0.5 - total / (2.0 * order), (1,))
    return (sign_next, occupation)


def solution(mesh):
    placed = (P(("ka", "row"), None),)
    return jax.shard_map(
        shards,
        mesh=mesh,
        in_specs=placed,
        out_specs=(P(("ka", "row"), None), P("ka")),
        check_vma=False,
    )
```

profile of v0, /device:TPU:0, one launch (start us, length us, event | category | flops | bytes accessed | tf_op | source)
XLA Modules:
  0.0 269.6 jit_solution(1665986670191946976)
XLA Ops:
  7.2 0.0 all-gather.2.cloned.1.call-start
  7.2 6.0 %convert_element_type.6 = bf16[512,4096]{1,0:T(8,128)(2,1)} convert(f32[512,4096]{1,0:T(8,128)} %param.1) | non-fusion elementwise | flops 2097152 | bytes 12582912 | tf_op jit(solution)/shard_map/convert_element_type | solution.py:22
  13.2 0.0 all-gather.2.cloned.1.call-update
  13.3 163.5 %all-gather.2.cloned.1.call-done = bf16[4096,4096]{1,0:T(8,128)(2,1)} async-done(((bf16[512,4096]{1,0:T(8,128)(2,1)}), bf16[4096,4096]{1,0:T(8,128)(2,1)}) %all-gather.2.cloned.1.call-update) | async-done | bytes 33554448 | tf_op jit(solution)/shard_map/all_gather | solution.py:23
  176.8 24.8 %convolution_convert_fusion.clone.4 = bf16[512,4096]{1,0:T(8,128)(2,1)} fusion(bf16[4096,4096]{1,0:T(8,128)(2,1)} %all-gather.2.cloned.1.call-done, f32[512,4096]{1,0:T(8,128)} %param.1), kind=kOutput, calls=%fused_computation.2.clone.clone.clone.1 | convolution fusion | flops 17184063488 | bytes 46137344 | tf_op jit(solution)/shard_map/dot_general | solution.py:9
  201.6 27.9 %multiply_subtract_fusion = f32[512,4096]{1,0:T(8,128)} fusion(f32[512,4096]{1,0:T(8,128)} %param.1, bf16[4096,4096]{1,0:T(8,128)(2,1)} %all-gather.2.cloned.1.call-done, bf16[512,4096]{1,0:T(8,128)(2,1)} %convolution_convert_fusion.clone.4), kind=kOutput, calls=%fused_computation.1 | convolution fusion | flops 17186160640 | bytes 54525952 | tf_op jit(solution)/shard_map/dot_general | solution.py:9
  229.5 11.5 %copy.4 = f32[64,8,8,512]{3,2,1,0:T(8,128)S(1)} copy(f32[64,8,8,512]{3,1,2,0:T(8,128)} %bitcast.17) | data formatting | bytes 16777216
  241.0 1.1 constant_dynamic-slice_fusion
  242.1 0.1 copy.6
  242.1 4.5 %gather_fusion = f32[512]{0:T(512)S(1)} fusion(f32[512,512]{1,0:T(8,128)S(1)} %bitcast.16, s32[512]{0:T(512)S(1)} %bitcast.14), kind=kCustom, calls=%fused_computation | custom fusion | bytes 8192 | tf_op jit(solution)/shard_map/jit(diagonal)/cond/branch_0_fun/gather | solution.py:15
  246.7 0.6 reduce_sum.9
  247.3 13.7 %psum.7 = f32[]{:T(128)} all-reduce(f32[]{:T(128)} %reduce_sum.9), channel_id=1, replica_groups=mesh['ka'=4,'row'=8] {'row'}, use_global_device_ids=true, to_apply=%region_1.2 | all-reduce | flops 1 | bytes 8 | tf_op jit(solution)/shard_map/psum | solution.py:28
  (1 shorter events, 0.0 us)
Async XLA Ops:
  7.2 169.6 %all-gather.2.cloned.1.call-start = ((), (), s32[]{:S(2)}) async-start(), calls=%async_computation | async-start | bytes 37748736 | tf_op jit(solution)/shard_map/all_gather | solution.py:23
Sparse Core Ops, SparseCore 0:
  13.4 163.3 all-gather.1
where the time goes:
time: 270 us
  waiting for transfers between devices  164 us (61%)
  matrix products  52.7 us (20%)
  local copies, waits for them, and re-layouts  17.1 us (6%)
  between operations  15.8 us (6%)
  blocking collectives  13.7 us (5%)
  other arithmetic  6.63 us (2%)
    all_gather x1, waiting for transfers between devices, shards(): gathered = lax.all_gather(rounded, 'row', axis=0, tiled=True)  164 us
    dot_general x2, matrix products, multiply_rows(): return jnp.dot(left, gathered, preferred_element_type=jnp.float32)  52.7 us
    psum x1, blocking collectives, shards(): lax.psum(own_diagonal(sign_next, position, block_rows, cycle_size), 'row')  13.7 us
    unnamed x2, local copies, waits for them, and re-layouts  11.6 us
    convert_element_type x1, other arithmetic, shards(): rounded = hamiltonian.astype(jnp.bfloat16)  6.03 us
  transfers between devices with their start and end apart: 1, of which 1 were waited for; matrix products, arithmetic and copies ran while one was open for 0% of the time, Pallas kernels for 0%

commit v1 on v0

--- a/solution.py
+++ b/solution.py
@@ -20,7 +20,12 @@
     position = lax.axis_index("row")
     block_rows, order = hamiltonian.shape
     rounded = hamiltonian.astype(jnp.bfloat16)
-    gathered = lax.all_gather(rounded, "row", axis=0, tiled=True)
+    ring = [rounded]
+    for hop in range(7):
+        ring.append(lax.ppermute(ring[-1], "row", [(dev, (dev + 1) % 8) for dev in range(8)]))
+    gathered = jnp.roll(
+        jnp.concatenate(ring[::-1], axis=0), (lax.axis_index("row") + 1) * ring[0].shape[0], axis=0
+    )
     multiply = partial(multiply_rows, gathered=gathered)
     square_low = multiply(rounded).astype(jnp.bfloat16)
     cube = multiply(square_low)

time: 270 us -> 504 us (1.87)
  waiting for transfers between devices: 164 us -> 342 us
  local copies, waits for them, and re-layouts: 17.1 us -> 79.4 us
  between operations: 15.8 us -> 2.51 us
  other arithmetic: 6.63 us -> 16.5 us
    ppermute x0 -> x7, waiting for transfers between devices: none -> 342 us  [shards(): lax.ppermute(ring[-1], 'row', [(dev, (dev + 1) % 8) for dev in range(8)])]
    all_gather x1 -> x0, waiting for transfers between devices: 164 us -> none  [shards(): gathered = lax.all_gather(rounded, 'row', axis=0, tiled=True)]
    unnamed x2 -> x36, local copies, waits for them, and re-layouts: 11.6 us -> 73.8 us
    concatenate x0 -> x1, other arithmetic: none -> 5.95 us  [shards(): jnp.roll(jnp.concatenate(ring[::-1], axis=0), (lax.axis_index('row') + 1)...]
    unnamed x0 -> x1, other arithmetic: none -> 5.93 us
  transfers between devices with their start and end apart: 1 -> 7, of which waited for: 1 -> 7; matrix products, arithmetic and copies ran while one was open for 0% -> 0% of each run, Pallas kernels for 0% -> 0%
where the time goes in v1:
time: 504 us
  waiting for transfers between devices  342 us (68%)
  local copies, waits for them, and re-layouts  79.4 us (16%)
  matrix products  49.9 us (10%)
  other arithmetic  16.5 us (3%)
  blocking collectives  12.4 us (2%)
    ppermute x7, waiting for transfers between devices, shards(): lax.ppermute(ring[-1], 'row', [(dev, (dev + 1) % 8) for dev in range(8)])  342 us
    unnamed x36, local copies, waits for them, and re-layouts  73.8 us
    dot_general x2, matrix products, multiply_rows(): return jnp.dot(left, gathered, preferred_element_type=jnp.float32)  49.9 us
    psum x1, blocking collectives, shards(): lax.psum(own_diagonal(sign_next, position, block_rows, cycle_size), 'row')  12.4 us
  transfers between devices with their start and end apart: 7, of which 7 were waited for; matrix products, arithmetic and copies ran while one was open for 0% of the time, Pallas kernels for 0%

profile of v1, /device:TPU:0, one launch (start us, length us, event | category | flops | bytes accessed | tf_op | source)
XLA Modules:
  0.0 503.7 jit_solution(15780450108629022856)
XLA Ops:
  0.6 4.0 convert_element_type.7
  4.6 0.5 collective-permute-start
  5.2 49.1 %collective-permute-done = bf16[512,4096]{1,0:T(8,128)(2,1)S(1)} collective-permute-done((bf16[512,4096]{1,0:T(8,128)(2,1)S(1)}, bf16[512,4096]{1,0:T(8,128)(2,1)S(1)}, u32[]{:S(2)}, u32[]{:S(2)}) %collective-permute-start) | collective-permute-done | bytes 4194336 | tf_op jit(solution)/shard_map/ppermute | solution.py:25
  54.2 0.0 copy-start
  54.2 2.0 copy-done
  56.2 0.0 collective-permute-start.1
  56.2 48.8 %collective-permute-done.1 = bf16[512,4096]{1,0:T(8,128)(2,1)S(1)} collective-permute-done((bf16[512,4096]{1,0:T(8,128)(2,1)S(1)}, bf16[512,4096]{1,0:T(8,128)(2,1)S(1)}, u32[]{:S(2)}, u32[]{:S(2)}) %collective-permute-start.1) | collective-permute-done | bytes 4194336 | tf_op jit(solution)/shard_map/ppermute | solution.py:25
  105.1 0.0 copy-start.2
  105.1 2.0 copy-done.2
  107.0 0.0 collective-permute-start.2
  107.0 48.8 %collective-permute-done.2 = bf16[512,4096]{1,0:T(8,128)(2,1)S(1)} collective-permute-done((bf16[512,4096]{1,0:T(8,128)(2,1)S(1)}, bf16[512,4096]{1,0:T(8,128)(2,1)S(1)}, u32[]{:S(2)}, u32[]{:S(2)}) %collective-permute-start.2) | collective-permute-done | bytes 4194336 | tf_op jit(solution)/shard_map/ppermute | solution.py:25
  155.9 0.0 copy-start.4
  155.9 2.0 copy-done.4
  157.9 0.0 collective-permute-start.3
  157.9 48.8 %collective-permute-done.3 = bf16[512,4096]{1,0:T(8,128)(2,1)S(1)} collective-permute-done((bf16[512,4096]{1,0:T(8,128)(2,1)S(1)}, bf16[512,4096]{1,0:T(8,128)(2,1)S(1)}, u32[]{:S(2)}, u32[]{:S(2)}) %collective-permute-start.3) | collective-permute-done | bytes 4194336 | tf_op jit(solution)/shard_map/ppermute | solution.py:25
  206.7 0.0 copy-start.6
  206.7 2.0 copy-done.6
  208.7 0.0 collective-permute-start.4
  208.7 48.8 %collective-permute-done.4 = bf16[512,4096]{1,0:T(8,128)(2,1)S(1)} collective-permute-done((bf16[512,4096]{1,0:T(8,128)(2,1)S(1)}, bf16[512,4096]{1,0:T(8,128)(2,1)S(1)}, u32[]{:S(2)}, u32[]{:S(2)}) %collective-permute-start.4) | collective-permute-done | bytes 4194336 | tf_op jit(solution)/shard_map/ppermute | solution.py:25
  257.5 0.0 copy-start.8
  257.5 2.0 copy-done.8
  259.5 0.0 collective-permute-start.5
  259.5 48.9 %collective-permute-done.5 = bf16[512,4096]{1,0:T(8,128)(2,1)} collective-permute-done((bf16[512,4096]{1,0:T(8,128)(2,1)S(1)}, bf16[512,4096]{1,0:T(8,128)(2,1)}, u32[]{:S(2)}, u32[]{:S(2)}) %collective-permute-start.5) | collective-permute-done | bytes 4194336 | tf_op jit(solution)/shard_map/ppermute | solution.py:25
  308.5 0.0 collective-permute-start.6
  308.5 0.0 copy-start.7
  308.5 0.0 copy-start.5
  308.5 0.0 copy-start.3
  308.5 0.0 copy-start.1
  308.5 49.1 %collective-permute-done.6 = bf16[512,4096]{1,0:T(8,128)(2,1)} collective-permute-done((bf16[512,4096]{1,0:T(8,128)(2,1)}, bf16[512,4096]{1,0:T(8,128)(2,1)}, u32[]{:S(2)}, u32[]{:S(2)}) %collective-permute-start.6) | collective-permute-done | bytes 4194336 | tf_op jit(solution)/shard_map/ppermute | solution.py:25
  357.6 4.6 constant_dynamic-update-slice_fusion.15
  362.2 4.7 constant_dynamic-update-slice_fusion.14
  366.9 4.6 constant_dynamic-update-slice_fusion.13
  371.5 4.6 constant_dynamic-update-slice_fusion.12
  376.2 4.6 constant_dynamic-update-slice_fusion.11
  380.8 4.6 constant_dynamic-update-slice_fusion.10
  385.4 4.6 constant_dynamic-update-slice_fusion.9
  390.1 5.9 %constant_dynamic-update-slice_fusion.8 = bf16[8192,4096]{1,0:T(8,128)(2,1)} fusion(bf16[8192,4096]{1,0:T(8,128)(2,1)} %constant_dynamic-update-slice_fusion.9, f32[512,4096]{1,0:T(8,128)} %param.1), kind=kLoop, calls=%fused_computation.16 | loop fusion | flops 2097152 | bytes 12582912
  396.0 4.7 constant_dynamic-update-slice_fusion.7
  400.8 4.6 constant_dynamic-update-slice_fusion.6
  405.4 4.6 constant_dynamic-update-slice_fusion.5
  410.0 0.0 copy-done.7
  410.0 2.2 constant_dynamic-update-slice_fusion.4
  412.2 0.0 copy-done.5
  412.2 2.3 constant_dynamic-update-slice_fusion.3
  414.6 0.0 copy-done.3
  414.6 2.2 constant_dynamic-update-slice_fusion.2
  416.8 0.0 copy-done.1
  416.8 2.2 constant_dynamic-update-slice_fusion.1
  419.0 6.0 %constant_dynamic-update-slice_fusion = bf16[8192,4096]{1,0:T(8,128)(2,1)} fusion(bf16[8192,4096]{1,0:T(8,128)(2,1)} %constant_dynamic-update-slice_fusion.1, f32[512,4096]{1,0:T(8,128)} %param.1), kind=kLoop, calls=%fused_computation.8 | loop fusion | flops 2097152 | bytes 12582912 | tf_op jit(solution)/shard_map/jit(_roll_dynamic)/concatenate | solution.py:26
  425.0 26.4 %fusion.6.clone.5 = bf16[4096,512]{1,0:T(8,128)(2,1)} fusion(bf16[8192,4096]{1,0:T(8,128)(2,1)} %constant_dynamic-update-slice_fusion, s32[]{:T(128)S(6)} %select_n.21, f32[512,4096]{1,0:T(8,128)} %param.1), kind=kOutput, calls=%fused_computation.6.clone.clone.clone.2 | convolution fusion | flops 17184063488 | bytes 46137348 | tf_op jit(solution)/shard_map/dot_general | solution.py:9
  451.4 23.5 %multiply_subtract_fusion = f32[512,4096]{1,0:T(8,128)S(1)} fusion(f32[512,4096]{1,0:T(8,128)} %param.1, bf16[8192,4096]{1,0:T(8,128)(2,1)} %constant_dynamic-update-slice_fusion, s32[]{:T(128)S(6)} %select_n.21, bf16[4096,512]{1,0:T(8,128)(2,1)} %fusion.6.clone.5), kind=kOutput, calls=%fused_computation.5 | convolution fusion | flops 17186160640 | bytes 54525956 | tf_op jit(solution)/shard_map/dot_general | solution.py:9
  474.9 0.0 copy-start.9
  474.9 8.3 %copy.4 = f32[64,8,8,512]{3,2,1,0:T(8,128)S(1)} copy(f32[64,8,8,512]{3,1,2,0:T(8,128)S(1)} %bitcast.16) | data formatting | bytes 16777216
  483.2 1.1 constant_dynamic-slice_fusion
  484.3 0.0 copy-done.9
  484.3 0.1 copy.6
  484.4 4.5 gather_fusion
  488.9 0.6 reduce_sum.9
  489.5 12.4 %psum.7 = f32[]{:T(128)} all-reduce(f32[]{:T(128)} %reduce_sum.9), channel_id=1, replica_groups=mesh['ka'=4,'row'=8] {'row'}, use_global_device_ids=true, to_apply=%region_1.2 | all-reduce | flops 1 | bytes 8 | tf_op jit(solution)/shard_map/psum | solution.py:33
  (1 shorter events, 0.0 us)
Async XLA Ops:
  4.6 49.6 %collective-permute-start = (bf16[512,4096]{1,0:T(8,128)(2,1)S(1)}, bf16[512,4096]{1,0:T(8,128)(2,1)S(1)}, u32[]{:S(2)}, u32[]{:S(2)}) collective-permute-start(bf16[512,4096]{1,0:T(8,128)(2,1)S(1)} %convert_element_type.7), channel_id=1, source_target_pairs={{0,1},{1,2},{2,3},{3,4},{4,5},{5,6},{6,7},{7,0},{8,9},{9,10},{10,1... | collective-permute-start | bytes 12582920 | tf_op jit(solution)/shard_map/ppermute | solution.py:25
  54.2 2.0 copy-start
  56.2 48.8 %collective-permute-start.1 = (bf16[512,4096]{1,0:T(8,128)(2,1)S(1)}, bf16[512,4096]{1,0:T(8,128)(2,1)S(1)}, u32[]{:S(2)}, u32[]{:S(2)}) collective-permute-start(bf16[512,4096]{1,0:T(8,128)(2,1)S(1)} %collective-permute-done), channel_id=1, source_target_pairs={{0,1},{1,2},{2,3},{3,4},{4,5},{5,6},{6,7},{7,0},{8,9},{9,10},{10,1... | collective-permute-start | bytes 12582920 | tf_op jit(solution)/shard_map/ppermute | solution.py:25
  105.1 2.0 copy-start.2
  107.0 48.8 %collective-permute-start.2 = (bf16[512,4096]{1,0:T(8,128)(2,1)S(1)}, bf16[512,4096]{1,0:T(8,128)(2,1)S(1)}, u32[]{:S(2)}, u32[]{:S(2)}) collective-permute-start(bf16[512,4096]{1,0:T(8,128)(2,1)S(1)} %collective-permute-done.1), channel_id=1, source_target_pairs={{0,1},{1,2},{2,3},{3,4},{4,5},{5,6},{6,7},{7,0},{8,9},{9,10},{10,1... | collective-permute-start | bytes 12582920 | tf_op jit(solution)/shard_map/ppermute | solution.py:25
  155.9 2.0 copy-start.4
  157.9 48.8 %collective-permute-start.3 = (bf16[512,4096]{1,0:T(8,128)(2,1)S(1)}, bf16[512,4096]{1,0:T(8,128)(2,1)S(1)}, u32[]{:S(2)}, u32[]{:S(2)}) collective-permute-start(bf16[512,4096]{1,0:T(8,128)(2,1)S(1)} %collective-permute-done.2), channel_id=1, source_target_pairs={{0,1},{1,2},{2,3},{3,4},{4,5},{5,6},{6,7},{7,0},{8,9},{9,10},{10,1... | collective-permute-start | bytes 12582920 | tf_op jit(solution)/shard_map/ppermute | solution.py:25
  206.7 2.0 copy-start.6
  208.7 48.8 %collective-permute-start.4 = (bf16[512,4096]{1,0:T(8,128)(2,1)S(1)}, bf16[512,4096]{1,0:T(8,128)(2,1)S(1)}, u32[]{:S(2)}, u32[]{:S(2)}) collective-permute-start(bf16[512,4096]{1,0:T(8,128)(2,1)S(1)} %collective-permute-done.3), channel_id=1, source_target_pairs={{0,1},{1,2},{2,3},{3,4},{4,5},{5,6},{6,7},{7,0},{8,9},{9,10},{10,1... | collective-permute-start | bytes 12582920 | tf_op jit(solution)/shard_map/ppermute | solution.py:25
  257.5 2.0 copy-start.8
  259.5 48.9 %collective-permute-start.5 = (bf16[512,4096]{1,0:T(8,128)(2,1)S(1)}, bf16[512,4096]{1,0:T(8,128)(2,1)}, u32[]{:S(2)}, u32[]{:S(2)}) collective-permute-start(bf16[512,4096]{1,0:T(8,128)(2,1)S(1)} %collective-permute-done.4), channel_id=1, source_target_pairs={{0,1},{1,2},{2,3},{3,4},{4,5},{5,6},{6,7},{7,0},{8,9},{9,10},{10,1... | collective-permute-start | bytes 12582920 | tf_op jit(solution)/shard_map/ppermute | solution.py:25
  308.5 49.1 %collective-permute-start.6 = (bf16[512,4096]{1,0:T(8,128)(2,1)}, bf16[512,4096]{1,0:T(8,128)(2,1)}, u32[]{:S(2)}, u32[]{:S(2)}) collective-permute-start(bf16[512,4096]{1,0:T(8,128)(2,1)} %collective-permute-done.5), channel_id=1, source_target_pairs={{0,1},{1,2},{2,3},{3,4},{4,5},{5,6},{6,7},{7,0},{8,9},{9,10},{10,1... | collective-permute-start | bytes 12582920 | tf_op jit(solution)/shard_map/ppermute | solution.py:25
  308.5 101.6 %copy-start.7 = (bf16[512,4096]{1,0:T(8,128)(2,1)S(1)}, bf16[512,4096]{1,0:T(8,128)(2,1)}, u32[]{:S(2)}) copy-start(bf16[512,4096]{1,0:T(8,128)(2,1)} %copy-done.6) | copy-start | bytes 12582916
  308.5 103.8 %copy-start.5 = (bf16[512,4096]{1,0:T(8,128)(2,1)S(1)}, bf16[512,4096]{1,0:T(8,128)(2,1)}, u32[]{:S(2)}) copy-start(bf16[512,4096]{1,0:T(8,128)(2,1)} %copy-done.4) | copy-start | bytes 12582916
  308.5 106.1 %copy-start.3 = (bf16[512,4096]{1,0:T(8,128)(2,1)S(1)}, bf16[512,4096]{1,0:T(8,128)(2,1)}, u32[]{:S(2)}) copy-start(bf16[512,4096]{1,0:T(8,128)(2,1)} %copy-done.2) | copy-start | bytes 12582916
  308.5 108.3 %copy-start.1 = (bf16[512,4096]{1,0:T(8,128)(2,1)S(1)}, bf16[512,4096]{1,0:T(8,128)(2,1)}, u32[]{:S(2)}) copy-start(bf16[512,4096]{1,0:T(8,128)(2,1)} %copy-done) | copy-start | bytes 12582916
  474.9 9.4 %copy-start.9 = (f32[512,4096]{1,0:T(8,128)}, f32[512,4096]{1,0:T(8,128)S(1)}, u32[]{:S(2)}) copy-start(f32[512,4096]{1,0:T(8,128)S(1)} %multiply_subtract_fusion) | copy-start | bytes 25165828
